TPU v7x, 256 devices: a whole 4x4x8 slice. The times are simulated.
256 devices in a mesh: dp: 8 (over y, core), vocab: 32 (over x, z).
Axes of the slice: x: 4, y: 4, z: 8, core: 2. Of those that a mesh axis runs over, the one named last changes fastest.
Arguments:
- student_hidden: bfloat16 [4096, 2048], P('dp', 'vocab'), may hold values from -150 to 150
- teacher_hidden: bfloat16 [4096, 2048], P('dp', 'vocab'), may hold values from -150 to 150
- head: bfloat16 [2048, 65536], P(None, 'vocab'), may hold values from -0.375 to 0.375
- mask: int32 [4096], P('dp'), may hold values from 0 to 1
- steps: int32 [32], P('dp'), may hold values from 1 to 8
Outputs:
- divergence: float32 [4096], P('dp')
- hidden_grad: bfloat16 [4096, 2048], P('dp', 'vocab')
All inputs are finite; a program needn't handle non-finite values.
Results may differ from a plain program's by a relative error of at most 0.0051.
Values may be sent and summed in bfloat16 or wider, within the bound.
No kernel may reach another device: no remote copies, remote signals or barrier semaphores. Data moves between devices by JAX's collectives and lax.ppermute only.
A program may use at most 64 MiB of HBM per device.

v0:
```python
import jax
import jax.numpy as jnp
from jax import lax
from jax.sharding import Mesh
from jax.sharding import PartitionSpec as P

LENGTH = 128
STEPS = 8
VOCAB = ("vocab_0", "vocab_1")


def sent_to_all(value, axis):
    copies = jnp.broadcast_to(value, (lax.axis_size(axis), *value.shape))
    return lax.all_to_all(copies, axis, split_axis=0, concat_axis=0, tiled=True)


def taken_together(value, axis):
    everything = sent_to_all(value, axis)
    return jnp.sum(everything, axis=0)


def gather_turned(arrays, axis, dims):
    turned = [jnp.moveaxis(a, dim, 0) for a, dim in zip(arrays, dims)]
    both = jnp.concatenate([t.reshape(len(t), -1) for t in turned], axis=1)
    whole, at, done = (lax.all_gather(both, axis, axis=0, tiled=True), 0, [])
    for t, dim in zip(turned, dims):
        piece = whole[:, at : at + t[0].size].reshape(-1, *t.shape[1:])
        done.append(jnp.moveaxis(piece, 0, dim))
        at += t[0].size
    return tuple(done)


def gathered_once(value, axis):
    leaves = jax.tree.leaves(value)
    order = sorted(range(len(leaves)), key=lambda k: -leaves[k].size)
    width = (1, *leaves[order[0]].shape)[-1]
    lines = [
        jnp.pad(leaves[k].reshape(-1), (0, -leaves[k].size % width)).reshape(-1, width)
        for k in order
    ]
    both, at, found = (sent_to_all(jnp.concatenate(lines), axis), 0, {})
    for k, line in zip(order, lines):
        piece = both[:, at : at + len(line)].reshape(len(both), -1)
        found[k] = piece[:, : leaves[k].size].reshape(-1, *leaves[k].shape)
        at += len(line)
    numbers = iter(range(len(leaves)))
    return jax.tree.map(lambda _: found[next(numbers)], value)


def joined_by_halves(pieces, combine):
    while len(jax.tree.leaves(pieces)[0]) > 1:
        pieces = jax.vmap(combine)(
            *(jax.tree.map(lambda part: part[side::2], pieces) for side in (0, 1))
        )
    return jax.tree.map(lambda part: part[0], pieces)


def merged_2(value, axis, combine):
    pieces = gathered_once(value, axis)
    return joined_by_halves(pieces, combine)


def own_rows(total, axes):
    for axis in axes:
        total = lax.psum_scatter(total, axis, scatter_dimension=0, tiled=True)
    return total


def combine_stats(former, latter):
    student_peak = jnp.maximum(former[0], latter[0])
    teacher_peak = jnp.maximum(former[2], latter[2])
    student_former = jnp.exp(former[0] - student_peak)
    student_latter = jnp.exp(latter[0] - student_peak)
    teacher_former = jnp.exp(former[2] - teacher_peak)
    teacher_latter = jnp.exp(latter[2] - teacher_peak)
    return (
        student_peak,
        former[1] * student_former + latter[1] * student_latter,
        teacher_peak,
        former[3] * teacher_former + latter[3] * teacher_latter,
        former[4] * teacher_former + latter[4] * teacher_latter,
    )


def per_device(student_hidden, teacher_hidden, head, mask, steps):
    rows = mask.shape[0]
    masked = mask.astype(jnp.float32)
    count = taken_together(jnp.sum(masked), "dp")
    factor = jnp.repeat(STEPS / steps.astype(jnp.float32), LENGTH)
    weight = masked * factor * (rows * lax.axis_size("dp") / jnp.maximum(count, 1.0))
    student_full, teacher_full = gather_turned((student_hidden, teacher_hidden), VOCAB, (1, 1))
    student_log = jnp.dot(student_full, head, preferred_element_type=jnp.float32)
    teacher_log = jnp.dot(teacher_full, head, preferred_element_type=jnp.float32)
    student_local = jnp.max(student_log, axis=1)
    teacher_local = jnp.max(teacher_log, axis=1)
    student_exp = jnp.exp(student_log - student_local[:, None])
    teacher_exp = jnp.exp(teacher_log - teacher_local[:, None])
    student_sum = jnp.sum(student_exp, axis=1)
    teacher_sum = jnp.sum(teacher_exp, axis=1)
    cross_sum = jnp.sum(teacher_exp * (teacher_log - student_log), axis=1)
    merged = merged_2(
        (student_local, student_sum, teacher_local, teacher_sum, cross_sum), VOCAB, combine_stats
    )
    student_peak, student_total, teacher_peak, teacher_total, cross = merged
    divergence = (
        cross / teacher_total
        - (teacher_peak + jnp.log(teacher_total))
        + (student_peak + jnp.log(student_total))
    )
    student_prob = student_exp * (jnp.exp(student_local - student_peak) / student_total)[:, None]
    teacher_prob = teacher_exp * (jnp.exp(teacher_local - teacher_peak) / teacher_total)[:, None]
    slopes = (weight[:, None] * (student_prob - teacher_prob)).astype(jnp.bfloat16)
    summed = own_rows(
        lax.dot_general(head, slopes, (((1,), (1,)), ((), ())), preferred_element_type=jnp.float32),
        VOCAB,
    )
    hidden_grad = summed.T.astype(jnp.bfloat16)
    return (divergence, hidden_grad)


def solution(mesh):
    torus = Mesh(mesh.devices.reshape(mesh.shape["dp"], 4, 8), ("dp", "vocab_0", "vocab_1"))
    in_specs = (P("dp", VOCAB), P("dp", VOCAB), P(None, VOCAB), P("dp"), P("dp"))
    out_specs = (P("dp"), P("dp", VOCAB))
    return jax.shard_map(
        per_device, mesh=torus, in_specs=in_specs, out_specs=out_specs, check_vma=False
    )
```

profile of v0, /device:TPU:2, one launch (start us, length us, event | category | flops | bytes accessed | tf_op | source)
XLA Modules:
  0.0 246.0 jit_solution(11770091090711310746)
XLA Ops:
  7.2 0.0 all-gather.2.cloned.1.call-start
  7.2 1.5 pad_maximum_fusion
  8.8 1.3 convert_reduce_fusion
  10.1 1.2 broadcast_in_dim.16
  11.3 4.5 %all-to-all-start.1 = ((f32[8,1,1]{2,1,0:T(1,128)}), f32[8,1,1]{2,1,0:T(1,128)S(1)}, u32[]{:S(2)}, u32[]{:S(2)}) async-start(f32[8,1,1]{2,1,0:T(1,128)} %broadcast_in_dim.16), calls=%async_computation.1 | async-start | bytes 8192 | tf_op jit(solution)/shard_map/all_to_all | solution.py:14
  15.8 78.2 %all-gather.2.cloned.1.call-done = bf16[2048,1024]{1,0:T(8,128)(2,1)} async-done(((bf16[64,1024]{1,0:T(8,128)(2,1)}), bf16[2048,1024]{1,0:T(8,128)(2,1)}) %all-gather.2.cloned.1.call-update) | async-done | bytes 4194320 | tf_op jit(solution)/shard_map/all_gather | solution.py:25
  94.0 7.9 %fusion.17 = (f32[512]{0:T(512)S(1)}, f32[512,2048]{1,0:T(8,128)S(1)}) fusion(bf16[2048,2048]{1,0:T(8,128)(2,1)} %param.7, bf16[2048,1024]{1,0:T(8,128)(2,1)} %all-gather.2.cloned.1.call-done), kind=kOutput, calls=%fused_computation.65 | convolution fusion | flops 4296015360 | bytes 14682112 | tf_op jit(solution)/shard_map/dot_general | solution.py:93
  101.9 8.7 %fusion.16 = (f32[512]{0:T(512)S(1)}, f32[512,2048]{1,0:T(8,128)S(1)}) fusion(bf16[2048,2048]{1,0:T(8,128)(2,1)} %param.7, bf16[2048,1024]{1,0:T(8,128)(2,1)S(1)} %copy-done.3), kind=kOutput, calls=%fused_computation.64 | convolution fusion | flops 4296015360 | bytes 14682112 | tf_op jit(solution)/shard_map/dot_general | solution.py:92
  110.7 2.1 multiply_reduce_fusion
  112.8 0.9 broadcast_in_dim.6
  113.7 6.9 %all-to-all-start = ((f32[32,5,512]{2,1,0:T(8,128)}), f32[32,5,512]{2,1,0:T(8,128)S(1)}, u32[]{:S(2)}, u32[]{:S(2)}) async-start(f32[32,5,512]{2,1,0:T(8,128)} %broadcast_in_dim.6), calls=%async_computation | async-start | bytes 1048576 | tf_op jit(solution)/shard_map/all_to_all | solution.py:14
  120.6 0.0 reduce-scatter.5.cloned.1.call-start
  120.7 0.6 reduce_sum.49
  122.0 0.1 fusion.14
  122.1 11.6 %all-to-all-done = f32[32,5,512]{2,1,0:T(8,128)S(1)} async-done(((f32[32,5,512]{2,1,0:T(8,128)}), f32[32,5,512]{2,1,0:T(8,128)S(1)}, u32[]{:S(2)}, u32[]{:S(2)}) %all-to-all-start) | async-done | bytes 327712 | tf_op jit(solution)/shard_map/all_to_all | solution.py:14
  133.6 0.2 fusion.15
  135.1 0.6 exponential_divide_fusion.1
  135.7 12.8 %convolution_bitcast_fusion = f32[2048,512]{0,1:T(8,128)} fusion(bf16[2048,2048]{1,0:T(8,128)(2,1)} %param.7, f32[512,2048]{1,0:T(8,128)} %copy-done, f32[512,2048]{1,0:T(8,128)} %copy-done.1, f32[512]{0:T(512)S(1)} %get-tuple-element.40, f32[512]{0:T(512)S(1)} %get-tuple-element.38, f32[512]{0:T(512)S(1)} %fusion.14, f32[512]{0:T(512)S(1)} %get-tuple-element.43, ...), kind=kOutput, calls=%fused_computation.6 | convolution fusion | flops 4302307328 | bytes 20981760 | tf_op jit(solution)/shard_map/dot_general | solution.py:114
  148.5 0.0 reduce-scatter.7.cloned.1.call-start
  148.6 46.3 %reduce-scatter.5.cloned.1.call-done = f32[512,512]{0,1:T(8,128)} async-done(((f32[2048,512]{0,1:T(8,128)}), f32[512,512]{0,1:T(8,128)}) %reduce-scatter.5.cloned.1.call-update) | async-done | bytes 1048592 | tf_op jit(solution)/shard_map/reduce_scatter | solution.py:65
  194.9 2.6 %copy.24 = f32[512,512]{1,0:T(8,128)} copy(f32[512,512]{0,1:T(8,128)} %reduce-scatter.5.cloned.1.call-done) | data formatting | bytes 2097152
  197.5 40.2 %reduce-scatter.7.cloned.1.call-done = f32[64,512]{1,0:T(8,128)} async-done(((f32[512,512]{1,0:T(8,128)}), f32[64,512]{1,0:T(8,128)}) %reduce-scatter.7.cloned.1.call-update) | async-done | bytes 131088
  237.7 1.0 copy.25
  238.7 0.7 copy.23
  (74 shorter events, 1.2 us)
Async XLA Ops:
  7.2 86.8 %all-gather.2.cloned.1.call-start = ((), (), s32[]{:S(2)}) async-start(), calls=%async_computation.4 | async-start | bytes 4325376 | tf_op jit(solution)/shard_map/all_gather | solution.py:25
  11.3 101.5 %all-to-all-start.1 = ((f32[8,1,1]{2,1,0:T(1,128)}), f32[8,1,1]{2,1,0:T(1,128)S(1)}, u32[]{:S(2)}, u32[]{:S(2)}) async-start(f32[8,1,1]{2,1,0:T(1,128)} %broadcast_in_dim.16), calls=%async_computation.1 | async-start | bytes 8192 | tf_op jit(solution)/shard_map/all_to_all | solution.py:14
  94.0 7.9 %copy-start.3 = (bf16[2048,1024]{1,0:T(8,128)(2,1)S(1)}, bf16[2048,1024]{1,0:T(8,128)(2,1)}, u32[]{:S(2)}) copy-start(bf16[2048,1024]{1,0:T(8,128)(2,1)} %all-gather.2.cloned.1.call-done) | copy-start | bytes 12582916
  101.9 8.7 %copy-start = (f32[512,2048]{1,0:T(8,128)}, f32[512,2048]{1,0:T(8,128)S(1)}, u32[]{:S(2)}) copy-start(f32[512,2048]{1,0:T(8,128)S(1)} %get-tuple-element.44) | copy-start | bytes 12582916
  110.6 2.2 copy-start.1
  110.6 10.0 %copy-start.4 = (s32[4]{0:T(128)S(1)}, s32[4]{0:T(128)}, u32[]{:S(2)}) copy-start(s32[4]{0:T(128)} %param.9) | copy-start | bytes 52
  110.6 11.3 %copy-start.2 = (s32[512]{0:T(512)S(1)}, s32[512]{0:T(512)}, u32[]{:S(2)}) copy-start(s32[512]{0:T(512)} %param.8) | copy-start | bytes 6148
  113.7 19.9 %all-to-all-start = ((f32[32,5,512]{2,1,0:T(8,128)}), f32[32,5,512]{2,1,0:T(8,128)S(1)}, u32[]{:S(2)}, u32[]{:S(2)}) async-start(f32[32,5,512]{2,1,0:T(8,128)} %broadcast_in_dim.6), calls=%async_computation | async-start | bytes 1048576 | tf_op jit(solution)/shard_map/all_to_all | solution.py:14
  120.6 74.3 %reduce-scatter.5.cloned.1.call-start = ((), (), s32[]{:S(2)}) async-start(), calls=%async_computation.5 | async-start | bytes 5242880 | tf_op jit(solution)/shard_map/reduce_scatter | solution.py:65
  148.5 89.1 %reduce-scatter.7.cloned.1.call-start = ((), (), s32[]{:S(2)}) async-start(), calls=%async_computation.6 | async-start | bytes 1179648
Sparse Core Ops, SparseCore 0:
  10.6 83.4 all-gather.1
  148.7 46.1 reduce-scatter.4
  197.6 40.0 reduce-scatter.6
where the time goes:
time: 246 us
  waiting for transfers between devices  176 us (72%)
  matrix products  29.4 us (12%)
  between operations  14.7 us (6%)
  starting transfers between devices  11.5 us (5%)
  local copies, waits for them, and re-layouts  7.61 us (3%)
  other arithmetic  6.51 us (3%)
    all_gather x1, waiting for transfers between devices, gather_turned(): whole, at, done = (lax.all_gather(both, axis, axis=0, tiled=True), 0, [])  78.2 us
    reduce_scatter x1, waiting for transfers between devices, own_rows(): total = lax.psum_scatter(total, axis, scatter_dimension=0, tiled=True)  46.3 us
    unnamed x4, waiting for transfers between devices  40.2 us
    dot_general x1, matrix products, per_device(): lax.dot_general(head, slopes, (((1,), (1,)), ((), ())), preferred_element...  12.8 us
    all_to_all x2, waiting for transfers between devices, sent_to_all(): return lax.all_to_all(copies, axis, split_axis=0, concat_axis=0, tiled=True)  11.6 us
    all_to_all x2, starting transfers between devices, sent_to_all(): return lax.all_to_all(copies, axis, split_axis=0, concat_axis=0, tiled=True)  11.3 us
    dot_general x1, matrix products, per_device(): jnp.dot(student_full, head, preferred_element_type=jnp.float32)  8.68 us
    dot_general x1, matrix products, per_device(): jnp.dot(teacher_full, head, preferred_element_type=jnp.float32)  7.88 us
  transfers between devices with their start and end apart: 5, of which 4 were waited for; matrix products, arithmetic and copies ran while one was open for 9% of the time, Pallas kernels for 0%

commit v1 on v0

--- a/solution.py
+++ b/solution.py
@@ -7,6 +7,12 @@
 LENGTH = 128
 STEPS = 8
 VOCAB = ("vocab_0", "vocab_1")
+
+
+def set_series_for(view, axis_id, along_dim):
+    return jnp.concatenate(
+        lax.all_to_all(jnp.stack(lax.axis_size(axis_id) * [view], axis=0), axis_id, 0, 0), along_dim
+    )
 
 
 def sent_to_all(value, axis):
@@ -22,7 +28,7 @@
 def gather_turned(arrays, axis, dims):
     turned = [jnp.moveaxis(a, dim, 0) for a, dim in zip(arrays, dims)]
     both = jnp.concatenate([t.reshape(len(t), -1) for t in turned], axis=1)
-    whole, at, done = (lax.all_gather(both, axis, axis=0, tiled=True), 0, [])
+    whole, at, done = (set_series_for(both, axis, 0), 0, [])
     for t, dim in zip(turned, dims):
         piece = whole[:, at : at + t[0].size].reshape(-1, *t.shape[1:])
         done.append(jnp.moveaxis(piece, 0, dim))

time: 246 us -> 280 us (1.14)
  waiting for transfers between devices: 176 us -> 195 us
  starting transfers between devices: 11.5 us -> 23.9 us
    all_to_all x0 -> x1, waiting for transfers between devices: none -> 93.9 us  [set_series_for(): lax.all_to_all(jnp.stack(lax.axis_size(axis_id) * [view], axis=0), axis_i...]
    all_gather x1 -> x0, waiting for transfers between devices: 78.2 us -> none  [gather_turned(): whole, at, done = (lax.all_gather(both, axis, axis=0, tiled=True), 0, [])]
    all_to_all x0 -> x1, starting transfers between devices: none -> 11.8 us  [set_series_for(): lax.all_to_all(jnp.stack(lax.axis_size(axis_id) * [view], axis=0), axis_i...]
    all_to_all x2, waiting for transfers between devices: 11.6 us -> 14.8 us  [sent_to_all(): return lax.all_to_all(copies, axis, split_axis=0, concat_axis=0, tiled=True)]
    unnamed x4 -> x3, waiting for transfers between devices: 40.2 us -> 40.2 us
  transfers between devices with their start and end apart: 5 -> 5, of which waited for: 4 -> 4; matrix products, arithmetic and copies ran while one was open for 9% -> 7% of each run, Pallas kernels for 0% -> 0%
where the time goes in v1:
time: 280 us; the launch traced here: 279 us
  waiting for transfers between devices  195 us (70%)
  matrix products  29.8 us (11%)
  starting transfers between devices  23.9 us (9%)
  between operations  15 us (5%)
  local copies, waits for them, and re-layouts  10.1 us (4%)
  other arithmetic  5.18 us (2%)
    all_to_all x1, waiting for transfers between devices, set_series_for(): lax.all_to_all(jnp.stack(lax.axis_size(axis_id) * [view], axis=0), axis_i...  93.9 us
    reduce_scatter x1, waiting for transfers between devices, own_rows(): total = lax.psum_scatter(total, axis, scatter_dimension=0, tiled=True)  46.4 us
    unnamed x3, waiting for transfers between devices  40.2 us
    all_to_all x2, waiting for transfers between devices, sent_to_all(): return lax.all_to_all(copies, axis, split_axis=0, concat_axis=0, tiled=True)  14.8 us
    dot_general x1, matrix products, per_device(): lax.dot_general(head, slopes, (((1,), (1,)), ((), ())), preferred_element...  12.8 us
    all_to_all x2, starting transfers between devices, sent_to_all(): return lax.all_to_all(copies, axis, split_axis=0, concat_axis=0, tiled=True)  12 us
    all_to_all x1, starting transfers between devices, set_series_for(): lax.all_to_all(jnp.stack(lax.axis_size(axis_id) * [view], axis=0), axis_i...  11.8 us
    dot_general x1, matrix products, per_device(): jnp.dot(student_full, head, preferred_element_type=jnp.float32)  9.26 us
  transfers between devices with their start and end apart: 5, of which 4 were waited for; matrix products, arithmetic and copies ran while one was open for 7% of the time, Pallas kernels for 0%

profile of v1, /device:TPU:2, one launch (start us, length us, event | category | flops | bytes accessed | tf_op | source)
XLA Modules:
  0.0 279.3 jit_solution(3821326270522966472)
XLA Ops:
  7.2 0.9 pad_maximum_fusion
  8.0 2.5 stack.2
  10.5 11.8 %all-to-all-start = ((bf16[32,64,1024]{2,1,0:T(8,128)(2,1)}), bf16[32,64,1024]{2,1,0:T(8,128)(2,1)}, u32[]{:S(2)}, u32[]{:S(2)}) async-start(bf16[32,64,1024]{2,1,0:T(8,128)(2,1)} %stack.2), calls=%async_computation | async-start | bytes 8388608 | tf_op jit(solution)/shard_map/all_to_all | solution.py:14
  22.3 0.6 convert_reduce_fusion
  22.9 93.9 %all-to-all-done = bf16[32,64,1024]{2,1,0:T(8,128)(2,1)} async-done(((bf16[32,64,1024]{2,1,0:T(8,128)(2,1)}), bf16[32,64,1024]{2,1,0:T(8,128)(2,1)}, u32[]{:S(2)}, u32[]{:S(2)}) %all-to-all-start) | async-done | bytes 4194336 | tf_op jit(solution)/shard_map/all_to_all | solution.py:14
  116.8 1.2 broadcast_in_dim.16
  118.1 4.5 %all-to-all-start.2 = ((f32[8,1,1]{2,1,0:T(1,128)}), f32[8,1,1]{2,1,0:T(1,128)S(1)}, u32[]{:S(2)}, u32[]{:S(2)}) async-start(f32[8,1,1]{2,1,0:T(1,128)} %broadcast_in_dim.16), calls=%async_computation.2 | async-start | bytes 8192 | tf_op jit(solution)/shard_map/all_to_all | solution.py:20
  122.5 7.8 %fusion.17 = (f32[512]{0:T(512)S(1)}, f32[512,2048]{1,0:T(8,128)S(1)}) fusion(bf16[2048,2048]{1,0:T(8,128)(2,1)} %param.7, bf16[2048,1024]{1,0:T(8,128)(2,1)} %bitcast.2), kind=kOutput, calls=%fused_computation.65 | convolution fusion | flops 4296015360 | bytes 14682112 | tf_op jit(solution)/shard_map/dot_general | solution.py:99
  130.3 9.3 %fusion.16 = (f32[512]{0:T(512)S(1)}, f32[512,2048]{1,0:T(8,128)S(1)}) fusion(bf16[2048,2048]{1,0:T(8,128)(2,1)} %param.7, bf16[2048,1024]{1,0:T(8,128)(2,1)} %bitcast.2), kind=kOutput, calls=%fused_computation.64 | convolution fusion | flops 4296015360 | bytes 14682112 | tf_op jit(solution)/shard_map/dot_general | solution.py:98
  139.6 2.1 multiply_reduce_fusion
  141.8 0.9 broadcast_in_dim.6
  142.7 7.5 %all-to-all-start.1 = ((f32[32,5,512]{2,1,0:T(8,128)}), f32[32,5,512]{2,1,0:T(8,128)S(1)}, u32[]{:S(2)}, u32[]{:S(2)}) async-start(f32[32,5,512]{2,1,0:T(8,128)} %broadcast_in_dim.6), calls=%async_computation.1 | async-start | bytes 1048576 | tf_op jit(solution)/shard_map/all_to_all | solution.py:20
  150.3 0.6 reduce_sum.49
  151.6 0.1 fusion.14
  151.7 14.8 %all-to-all-done.1 = f32[32,5,512]{2,1,0:T(8,128)S(1)} async-done(((f32[32,5,512]{2,1,0:T(8,128)}), f32[32,5,512]{2,1,0:T(8,128)S(1)}, u32[]{:S(2)}, u32[]{:S(2)}) %all-to-all-start.1) | async-done | bytes 327712 | tf_op jit(solution)/shard_map/all_to_all | solution.py:20
  166.4 0.2 fusion.15
  168.0 0.6 exponential_divide_fusion.1
  168.5 12.8 %convolution_bitcast_fusion = f32[2048,512]{0,1:T(8,128)} fusion(bf16[2048,2048]{1,0:T(8,128)(2,1)} %param.7, f32[512,2048]{1,0:T(8,128)} %copy-done, f32[512,2048]{1,0:T(8,128)} %copy-done.1, f32[512]{0:T(512)S(1)} %get-tuple-element.40, f32[512]{0:T(512)S(1)} %get-tuple-element.38, f32[512]{0:T(512)S(1)} %fusion.14, f32[512]{0:T(512)S(1)} %get-tuple-element.43, ...), kind=kOutput, calls=%fused_computation.6 | convolution fusion | flops 4302307328 | bytes 20981760 | tf_op jit(solution)/shard_map/dot_general | solution.py:120
  181.4 0.0 reduce-scatter.7.cloned.1.call-start
  181.4 46.4 %reduce-scatter.5.cloned.1.call-done = f32[512,512]{0,1:T(8,128)} async-done(((f32[2048,512]{0,1:T(8,128)}), f32[512,512]{0,1:T(8,128)}) %reduce-scatter.5.cloned.1.call-update) | async-done | bytes 1048592 | tf_op jit(solution)/shard_map/reduce_scatter | solution.py:71
  227.9 2.6 copy.24
  230.5 40.2 %reduce-scatter.7.cloned.1.call-done = f32[64,512]{1,0:T(8,128)} async-done(((f32[512,512]{1,0:T(8,128)}), f32[64,512]{1,0:T(8,128)}) %reduce-scatter.7.cloned.1.call-update) | async-done | bytes 131088
  270.7 1.0 copy.25
  271.7 0.7 copy.23
  (72 shorter events, 1.3 us)
Async XLA Ops:
  10.5 11.8 %copy-start.2 = (s32[512]{0:T(512)S(1)}, s32[512]{0:T(512)}, u32[]{:S(2)}) copy-start(s32[512]{0:T(512)} %param.8) | copy-start | bytes 6148
  10.5 106.3 %all-to-all-start = ((bf16[32,64,1024]{2,1,0:T(8,128)(2,1)}), bf16[32,64,1024]{2,1,0:T(8,128)(2,1)}, u32[]{:S(2)}, u32[]{:S(2)}) async-start(bf16[32,64,1024]{2,1,0:T(8,128)(2,1)} %stack.2), calls=%async_computation | async-start | bytes 8388608 | tf_op jit(solution)/shard_map/all_to_all | solution.py:14
  118.1 23.7 %all-to-all-start.2 = ((f32[8,1,1]{2,1,0:T(1,128)}), f32[8,1,1]{2,1,0:T(1,128)S(1)}, u32[]{:S(2)}, u32[]{:S(2)}) async-start(f32[8,1,1]{2,1,0:T(1,128)} %broadcast_in_dim.16), calls=%async_computation.2 | async-start | bytes 8192 | tf_op jit(solution)/shard_map/all_to_all | solution.py:20
  130.3 9.3 %copy-start = (f32[512,2048]{1,0:T(8,128)}, f32[512,2048]{1,0:T(8,128)S(1)}, u32[]{:S(2)}) copy-start(f32[512,2048]{1,0:T(8,128)S(1)} %get-tuple-element.44) | copy-start | bytes 12582916
  139.6 2.2 copy-start.1
  139.6 10.7 %copy-start.3 = (s32[4]{0:T(128)S(1)}, s32[4]{0:T(128)}, u32[]{:S(2)}) copy-start(s32[4]{0:T(128)} %param.9) | copy-start | bytes 52
  142.7 23.8 %all-to-all-start.1 = ((f32[32,5,512]{2,1,0:T(8,128)}), f32[32,5,512]{2,1,0:T(8,128)S(1)}, u32[]{:S(2)}, u32[]{:S(2)}) async-start(f32[32,5,512]{2,1,0:T(8,128)} %broadcast_in_dim.6), calls=%async_computation.1 | async-start | bytes 1048576 | tf_op jit(solution)/shard_map/all_to_all | solution.py:20
  150.2 77.6 %reduce-scatter.5.cloned.1.call-start = ((), (), s32[]{:S(2)}) async-start(), calls=%async_computation.5 | async-start | bytes 5242880 | tf_op jit(solution)/shard_map/reduce_scatter | solution.py:71
  181.4 89.3 %reduce-scatter.7.cloned.1.call-start = ((), (), s32[]{:S(2)}) async-start(), calls=%async_computation.6 | async-start | bytes 1179648
Sparse Core Ops, SparseCore 0:
  181.5 46.3 reduce-scatter.4
  230.6 40.0 reduce-scatter.6
